TPU v7x, 32 devices: a whole 2x2x4 slice. The times are simulated.
32 devices in a mesh: group: 8 (over z, core), helper: 4 (over y, x).
Axes of the slice: x: 2, y: 2, z: 4, core: 2. Of those that a mesh axis runs over, the one named last changes fastest.
Arguments:
- candidates: bfloat16 [64, 128, 1024], P(('group', 'helper')), may hold values from -36 to 36
- block_user: int32 [64], P(('group', 'helper')), may hold values from 0 to 3, as said below
- live_rows: int32 [64], P(('group', 'helper')), may hold values from 1 to 128
- prefix_keys: bfloat16 [32, 256, 1024], P(('group', 'helper')), may hold values from -6 to 6
- prefix_values: bfloat16 [32, 256, 1024], P(('group', 'helper')), may hold values from -6 to 6
- w_proj: bfloat16 [1024, 4096], P(('group', 'helper')), may hold values from -0.1875 to 0.1875
- w_out: bfloat16 [1024, 1024], P(('group', 'helper')), may hold values from -0.1875 to 0.1875
- gain_in: float32 [1024], replicated, may hold values from 0.1 to 1.9
- gain_mid: float32 [1024], replicated, may hold values from 0.1 to 1.9
- score_vec: float32 [1024], replicated, may hold values from -0.1875 to 0.1875
Outputs:
- embeddings: bfloat16 [64, 128, 1024], P(('group', 'helper'))
- scores: float32 [64, 128], P(('group', 'helper'))
Inputs may be any that keep to these rules, and one draw needn't show every extreme that they name: `block_user`: the 2 blocks of one device name different users; in every group some user is named by a block of every device of the group.
All inputs are finite; a program needn't handle non-finite values.
Results may differ from a plain program's by a relative error of at most 0.0045.
Values may be sent and summed in bfloat16 or wider, within the bound.
No kernel may reach another device: no remote copies, remote signals or barrier semaphores. Data moves between devices by JAX's collectives and lax.ppermute only.
A program may use at most 128 MiB of HBM per device.

v0:
```python
import jax
import jax.numpy as jnp
from jax import lax
from jax.sharding import PartitionSpec as P

HEADS = 8
epsilon = 1e-05


def layer_norm(values, gain):
    average = jnp.mean(values, axis=-1, keepdims=True)
    centred = values - average
    spread = jnp.mean(centred * centred, axis=-1, keepdims=True)
    return centred * lax.rsqrt(spread + epsilon) * gain


def shards(
    candidates,
    block_user,
    live_rows,
    prefix_keys,
    prefix_values,
    w_proj,
    w_out,
    gain_in,
    gain_mid,
    score_vec,
):
    helpers = lax.axis_size("helper")
    blocks, rows_block, features = candidates.shape
    head_dim = features // HEADS
    score_scale = head_dim ** (-0.5)
    proj_full, out_full = (
        lax.all_gather(w_proj, ("group", "helper"), axis=0, tiled=True),
        lax.all_gather(w_out, ("group", "helper"), axis=0, tiled=True),
    )
    cand_rows = candidates.reshape(blocks * rows_block, features).astype(jnp.float32)
    normed = layer_norm(cand_rows, gain_in).astype(jnp.bfloat16)
    projected = jax.nn.silu(jnp.dot(normed, proj_full, preferred_element_type=jnp.float32))
    gate_portion = projected[:, :features]
    value_part = projected[:, features : 2 * features]
    query_portion = projected[:, 2 * features : 3 * features]
    key_part = projected[:, 3 * features :]
    query_bf = lax.optimization_barrier(query_portion.astype(jnp.bfloat16))
    query_heads = query_bf.astype(jnp.float32).reshape(-1, HEADS, head_dim)
    own_weight = jax.nn.silu(
        score_scale * jnp.sum(query_heads * key_part.reshape(-1, HEADS, head_dim), axis=-1)
    )
    own_term = (own_weight[..., None] * value_part.reshape(-1, HEADS, head_dim)).reshape(
        -1, features
    )
    onehot = (block_user[None, :] == jnp.arange(helpers, dtype=jnp.int32)[:, None]).astype(
        jnp.bfloat16
    )
    outgoing = jnp.dot(
        onehot, query_bf.reshape(blocks, rows_block * features), preferred_element_type=jnp.float32
    )
    outgoing = outgoing.astype(jnp.bfloat16).reshape(helpers, rows_block, features)
    per_head_keys = prefix_keys[0].reshape(-1, HEADS, head_dim)
    per_head_values = prefix_values[0].reshape(-1, HEADS, head_dim)

    def attended_row_set(query_tile_group):
        raw_scores = jnp.einsum(
            "ocy,qcy->coq", query_tile_group, per_head_keys, preferred_element_type=jnp.float32
        )
        weight_brainfloat = jax.nn.silu(score_scale * raw_scores).astype(jnp.bfloat16)
        return jnp.einsum(
            "txw,wta->xta", weight_brainfloat, per_head_values, preferred_element_type=jnp.float32
        ).astype(jnp.bfloat16)

    arrived = lax.all_to_all(outgoing, "helper", split_axis=0, concat_axis=0, tiled=True)
    arrived_shape = arrived.shape
    count_rows = arrived_shape[0] * arrived_shape[1]
    flat_query = arrived.reshape(count_rows, HEADS, head_dim)
    if count_rows > 512 and count_rows % 512 == 0:
        mixed_heads = lax.map(
            attended_row_set, flat_query.reshape(count_rows // 512, 512, HEADS, head_dim)
        )
    else:
        mixed_heads = attended_row_set(flat_query)
    returned = lax.all_to_all(
        mixed_heads.reshape(arrived_shape), "helper", split_axis=0, concat_axis=0, tiled=True
    )
    prefix_mix = jnp.einsum(
        "jb,jf->bf",
        onehot,
        returned.reshape(helpers, rows_block * features),
        preferred_element_type=jnp.float32,
    )
    mixed = prefix_mix.reshape(-1, features) + own_term
    gated = (layer_norm(mixed, gain_mid) * gate_portion).astype(jnp.bfloat16)
    updated = cand_rows + jnp.dot(gated, out_full, preferred_element_type=jnp.float32)
    embeddings = updated.astype(jnp.bfloat16).reshape(blocks, rows_block, features)
    row_scores = jnp.sum(layer_norm(updated, 1.0) * score_vec, axis=-1).reshape(blocks, rows_block)
    live_mask = jnp.arange(rows_block, dtype=jnp.int32)[None, :] < live_rows[:, None]
    scores = jnp.where(live_mask, row_scores, jnp.zeros_like(row_scores))
    return (embeddings, scores)


def solution(mesh):
    placed = (
        P(("group", "helper"), None, None),
        P(("group", "helper")),
        P(("group", "helper")),
        P(("group", "helper"), None, None),
        P(("group", "helper"), None, None),
        P(("group", "helper"), None),
        P(("group", "helper"), None),
        P(),
        P(),
        P(),
    )
    return jax.shard_map(
        shards,
        mesh=mesh,
        in_specs=placed,
        out_specs=(P(("group", "helper"), None, None), P(("group", "helper"), None)),
        check_vma=False,
    )
```

profile of v0, /device:TPU:0, one launch (start us, length us, event | category | flops | bytes accessed | tf_op | source)
XLA Modules:
  0.0 164.2 jit_solution(251757091519188598)
XLA Ops:
  7.2 0.0 all-gather.3.cloned.1.call-start
  7.2 0.7 all-gather.3.cloned.1.call-update
  7.9 0.0 all-gather.5.cloned.1.call-start
  7.9 0.7 all-gather.5.cloned.1.call-update
  8.6 1.2 convert_reduce_fusion
  9.8 1.3 multiply_reduce_fusion.3
  11.2 1.3 fusion.8
  12.5 0.0 copy-start.6
  12.5 78.1 %all-gather.3.cloned.1.call-done = bf16[1024,4096]{1,0:T(8,128)(2,1)} async-done(((bf16[32,4096]{1,0:T(8,128)(2,1)}), bf16[1024,4096]{1,0:T(8,128)(2,1)}) %all-gather.3.cloned.1.call-update) | async-done | bytes 8388624 | tf_op jit(solution)/shard_map/all_gather | solution.py:34
  90.7 5.9 %divide_multiply_fusion = f32[256,4096]{1,0:T(8,128)S(1)} fusion(bf16[256,1024]{1,0:T(8,128)(2,1)S(1)} %fusion.8, bf16[1024,4096]{1,0:T(8,128)(2,1)} %all-gather.3.cloned.1.call-done), kind=kOutput, calls=%fused_computation.2 | convolution fusion | flops 2151677952 | bytes 13107200 | tf_op jit(solution)/shard_map/dot_general | solution.py:39
  96.5 0.0 copy-start.1
  96.5 1.9 %copy-done.1 = f32[256,4096]{1,0:T(8,128)} copy-done((f32[256,4096]{1,0:T(8,128)}, f32[256,4096]{1,0:T(8,128)S(1)}, u32[]{:S(2)}) %copy-start.1) | copy-done | bytes 4194328
  98.5 0.1 slice.30
  98.5 0.4 reshape.106
  98.9 0.0 copy-start.2
  98.9 0.0 copy-start.3
  99.0 0.7 convolution_convert_fusion
  99.7 1.3 copy.47
  100.9 3.5 %all-to-all-start = ((bf16[4,128,1024]{2,1,0:T(8,128)(2,1)}), bf16[4,128,1024]{2,1,0:T(8,128)(2,1)S(1)}, u32[]{:S(2)}, u32[]{:S(2)}) async-start(bf16[4,128,1024]{2,1,0:T(8,128)(2,1)} %bitcast.46), calls=%async_computation | async-start | bytes 2097152 | tf_op jit(solution)/shard_map/all_to_all | solution.py:71
  104.5 0.1 copy.31
  104.6 0.0 copy-done.3
  104.6 0.9 copy.32
  105.5 13.3 %all-to-all-done = bf16[4,128,1024]{2,1,0:T(8,128)(2,1)S(1)} async-done(((bf16[4,128,1024]{2,1,0:T(8,128)(2,1)}), bf16[4,128,1024]{2,1,0:T(8,128)(2,1)S(1)}, u32[]{:S(2)}, u32[]{:S(2)}) %all-to-all-start) | async-done | bytes 1048608 | tf_op jit(solution)/shard_map/all_to_all | solution.py:71
  118.8 0.3 copy.30
  119.0 3.8 %fusion.2 = bf16[512,8,128]{2,0,1:T(8,128)(2,1)} fusion(bf16[512,8,128]{2,1,0:T(8,128)(2,1)S(1)} %bitcast.53, bf16[256,8,128]{2,1,0:T(8,128)(2,1)} %bitcast.59, bf16[256,8,128]{2,1,0:T(8,128)(2,1)S(1)} %bitcast.58), kind=kOutput, calls=%fused_computation.5 | convolution fusion | flops 543686656 | bytes 3145728 | tf_op jit(solution)/shard_map/txw,wta->xta/dot_general | solution.py:67
  122.9 1.9 %copy.26 = bf16[512,8,128]{2,1,0:T(8,128)(2,1)S(1)} copy(bf16[512,8,128]{2,0,1:T(8,128)(2,1)} %fusion.2) | data formatting | bytes 2097152 | tf_op jit(solution)/shard_map/convert_element_type | solution.py:69
  124.8 1.3 reshape.109
  126.1 3.7 %all-to-all-start.1 = ((bf16[4,128,1024]{2,1,0:T(8,128)(2,1)}), bf16[4,128,1024]{2,1,0:T(8,128)(2,1)S(1)}, u32[]{:S(2)}, u32[]{:S(2)}) async-start(bf16[4,128,1024]{2,1,0:T(8,128)(2,1)} %reshape.109), calls=%async_computation.1 | async-start | bytes 2097152 | tf_op jit(solution)/shard_map/all_to_all | solution.py:81
  129.8 1.4 fusion.5
  131.2 0.2 copy.34
  131.4 0.3 reduce_sum.74
  131.7 0.1 copy.27
  131.8 0.1 copy.28
  131.9 14.8 %all-to-all-done.1 = bf16[4,128,1024]{2,1,0:T(8,128)(2,1)S(1)} async-done(((bf16[4,128,1024]{2,1,0:T(8,128)(2,1)}), bf16[4,128,1024]{2,1,0:T(8,128)(2,1)S(1)}, u32[]{:S(2)}, u32[]{:S(2)}) %all-to-all-start.1) | async-done | bytes 1048608 | tf_op jit(solution)/shard_map/all_to_all | solution.py:81
  146.7 0.8 copy.33
  147.5 1.1 fusion.18
  148.6 0.0 copy-start
  148.6 0.0 copy-start.4
  148.7 0.9 reshape.111
  149.6 0.3 mul.124
  149.9 1.6 fusion.24
  151.5 0.2 multiply_reduce_fusion.2
  151.8 0.9 all-gather.5.cloned.1.call-done
  152.6 2.8 %fusion.26 = (f32[256]{0:T(256)S(1)}, f32[256,1024]{1,0:T(8,128)S(1)}) fusion(bf16[1024,1024]{1,0:T(8,128)(2,1)} %all-gather.5.cloned.1.call-done, f32[256,4096]{1,0:T(8,128)} %copy-done.1, f32[256,1024]{1,0:T(8,128)S(1)} %get-tuple-element.3, f32[1024]{0:T(1024)S(1)} %copy-done.4, f32[256]{0:T(256)S(1)} %add_rsqrt_fusion.1, ...), kind=kOutput, calls=%fused_computation.46 | convolution fusion | flops 538967808 | bytes 5774336 | tf_op jit(solution)/shard_map/dot_general | solution.py:92
  155.4 0.3 multiply_reduce_fusion.1
  155.7 0.0 copy-done.5
  155.7 1.1 multiply_reduce_fusion
  156.8 0.6 compare_select_fusion
  (14 shorter events, 0.1 us)
Async XLA Ops:
  7.2 83.5 %all-gather.3.cloned.1.call-start = ((), (), s32[]{:S(2)}) async-start(), calls=%async_computation.2 | async-start | bytes 8650752 | tf_op jit(solution)/shard_map/all_gather | solution.py:34
  7.9 144.7 %all-gather.5.cloned.1.call-start = ((), (), s32[]{:S(2)}) async-start(), calls=%async_computation.3 | async-start | bytes 2162688 | tf_op jit(solution)/shard_map/all_gather | solution.py:35
  12.5 86.4 %copy-start.6 = (s32[2]{0:T(128)S(1)}, s32[2]{0:T(128)}, u32[]{:S(2)}) copy-start(s32[2]{0:T(128)} %param.11) | copy-start | bytes 28
  96.5 1.9 %copy-start.1 = (f32[256,4096]{1,0:T(8,128)}, f32[256,4096]{1,0:T(8,128)S(1)}, u32[]{:S(2)}) copy-start(f32[256,4096]{1,0:T(8,128)S(1)} %divide_multiply_fusion) | copy-start | bytes 12582916
  98.9 5.5 %copy-start.2 = (bf16[1,256,1024]{2,1,0:T(8,128)(2,1)S(1)}, bf16[1,256,1024]{2,1,0:T(8,128)(2,1)}, u32[]{:S(2)}) copy-start(bf16[1,256,1024]{2,1,0:T(8,128)(2,1)} %param.13) | copy-start | bytes 1572868
  98.9 5.6 %copy-start.3 = (bf16[1,256,1024]{2,1,0:T(8,128)(2,1)S(1)}, bf16[1,256,1024]{2,1,0:T(8,128)(2,1)}, u32[]{:S(2)}) copy-start(bf16[1,256,1024]{2,1,0:T(8,128)(2,1)} %param.14) | copy-start | bytes 1572868
  100.9 17.8 %all-to-all-start = ((bf16[4,128,1024]{2,1,0:T(8,128)(2,1)}), bf16[4,128,1024]{2,1,0:T(8,128)(2,1)S(1)}, u32[]{:S(2)}, u32[]{:S(2)}) async-start(bf16[4,128,1024]{2,1,0:T(8,128)(2,1)} %bitcast.46), calls=%async_computation | async-start | bytes 2097152 | tf_op jit(solution)/shard_map/all_to_all | solution.py:71
  126.1 20.6 %all-to-all-start.1 = ((bf16[4,128,1024]{2,1,0:T(8,128)(2,1)}), bf16[4,128,1024]{2,1,0:T(8,128)(2,1)S(1)}, u32[]{:S(2)}, u32[]{:S(2)}) async-start(bf16[4,128,1024]{2,1,0:T(8,128)(2,1)} %reshape.109), calls=%async_computation.1 | async-start | bytes 2097152 | tf_op jit(solution)/shard_map/all_to_all | solution.py:81
  148.6 4.0 %copy-start = (bf16[2,128,1024]{2,1,0:T(8,128)(2,1)S(1)}, bf16[2,128,1024]{2,1,0:T(8,128)(2,1)}, u32[]{:S(2)}) copy-start(bf16[2,128,1024]{2,1,0:T(8,128)(2,1)} %param.10) | copy-start | bytes 1572868
  148.6 4.0 %copy-start.4 = (f32[1024]{0:T(1024)S(1)}, f32[1024]{0:T(1024)}, u32[]{:S(2)}) copy-start(f32[1024]{0:T(1024)} %param.18) | copy-start | bytes 12292
  151.5 4.2 %copy-start.5 = (f32[1024]{0:T(1024)S(1)}, f32[1024]{0:T(1024)}, u32[]{:S(2)}) copy-start(f32[1024]{0:T(1024)} %param.19) | copy-start | bytes 12292
  152.6 4.1 %copy-start.7 = (s32[2]{0:T(128)S(1)}, s32[2]{0:T(128)}, u32[]{:S(2)}) copy-start(s32[2]{0:T(128)} %param.12) | copy-start | bytes 28
Sparse Core Ops, SparseCore 0:
  10.8 79.7 all-gather.2
  93.5 59.0 all-gather.4
where the time goes:
time: 165 us; the launch traced here: 164 us
  waiting for transfers between devices  108 us (65%)
  matrix products  14.3 us (9%)
  between operations  14.3 us (9%)
  local copies, waits for them, and re-layouts  10.6 us (6%)
  other arithmetic  9.38 us (6%)
  starting transfers between devices  7.29 us (4%)
    all_gather x1, waiting for transfers between devices, shards(): lax.all_gather(w_proj, ('group', 'helper'), axis=0, tiled=True)  78.1 us
    all_to_all x1, waiting for transfers between devices, shards(): lax.all_to_all(mixed_heads.reshape(arrived_shape), 'helper', split_axis=0...  14.8 us
    all_to_all x1, waiting for transfers between devices, shards(): lax.all_to_all(outgoing, 'helper', split_axis=0, concat_axis=0, tiled=True)  13.3 us
    dot_general x1, matrix products, shards(): jnp.dot(normed, proj_full, preferred_element_type=jnp.float32)  5.86 us
    unnamed x22, local copies, waits for them, and re-layouts  5.51 us
    dot_general x1, matrix products, attended_row_set(): jnp.einsum('txw,wta->xta', weight_brainfloat, per_head_values, preferred_...  3.85 us
    all_to_all x1, starting transfers between devices, shards(): lax.all_to_all(mixed_heads.reshape(arrived_shape), 'helper', split_axis=0...  3.7 us
    all_to_all x1, starting transfers between devices, shards(): lax.all_to_all(outgoing, 'helper', split_axis=0, concat_axis=0, tiled=True)  3.51 us
  transfers between devices with their start and end apart: 4, of which 4 were waited for; matrix products, arithmetic and copies ran while one was open for 17% of the time, Pallas kernels for 0%

commit v1 on v0

--- a/solution.py
+++ b/solution.py
@@ -31,7 +31,12 @@
     head_dim = features // HEADS
     score_scale = head_dim ** (-0.5)
     proj_full, out_full = (
-        lax.all_gather(w_proj, ("group", "helper"), axis=0, tiled=True),
+        jnp.concatenate(
+            lax.all_to_all(
+                jnp.stack([w_proj] * lax.axis_size(("group", "helper"))), ("group", "helper"), 0, 0
+            ),
+            axis=0,
+        ),
         lax.all_gather(w_out, ("group", "helper"), axis=0, tiled=True),
     )
     cand_rows = candidates.reshape(blocks * rows_block, features).astype(jnp.float32)

time: 165 us -> 285 us (1.73)
  waiting for transfers between devices: 108 us -> 217 us
  starting transfers between devices: 7.29 us -> 14.7 us
  local copies, waits for them, and re-layouts: 10.6 us -> 16.6 us
  other arithmetic: 9.38 us -> 6.25 us
    all_to_all x0 -> x1, waiting for transfers between devices: none -> 194 us  [shards(): lax.all_to_all(jnp.stack([w_proj] * lax.axis_size(('group', 'helper'))),...]
    all_gather x1 -> x0, waiting for transfers between devices: 78.1 us -> none  [shards(): lax.all_gather(w_proj, ('group', 'helper'), axis=0, tiled=True)]
    all_to_all x0 -> x1, starting transfers between devices: none -> 7.45 us  [shards(): lax.all_to_all(jnp.stack([w_proj] * lax.axis_size(('group', 'helper'))),...]
    another operation x0 -> x1, local copies, waits for them, and re-layouts: none -> 5.21 us  [shards(): jnp.stack([w_proj] * lax.axis_size(('group', 'helper')))]
    all_to_all x1, waiting for transfers between devices: 14.8 us -> 10.8 us  [shards(): lax.all_to_all(mixed_heads.reshape(arrived_shape), 'helper', split_axis=0...]
    unnamed x22 -> x24, local copies, waits for them, and re-layouts: 5.51 us -> 6.32 us
  transfers between devices with their start and end apart: 4 -> 4, of which waited for: 4 -> 3; matrix products, arithmetic and copies ran while one was open for 17% -> 9% of each run, Pallas kernels for 0% -> 0%
where the time goes in v1:
time: 285 us; the launch traced here: 283 us
  waiting for transfers between devices  217 us (76%)
  local copies, waits for them, and re-layouts  16.6 us (6%)
  starting transfers between devices  14.7 us (5%)
  matrix products  14.4 us (5%)
  between operations  14.3 us (5%)
  other arithmetic  6.25 us (2%)
    all_to_all x1, waiting for transfers between devices, shards(): lax.all_to_all(jnp.stack([w_proj] * lax.axis_size(('group', 'helper'))),...  194 us
    all_to_all x1, waiting for transfers between devices, shards(): lax.all_to_all(outgoing, 'helper', split_axis=0, concat_axis=0, tiled=True)  11.8 us
    all_to_all x1, waiting for transfers between devices, shards(): lax.all_to_all(mixed_heads.reshape(arrived_shape), 'helper', split_axis=0...  10.8 us
    all_to_all x1, starting transfers between devices, shards(): lax.all_to_all(jnp.stack([w_proj] * lax.axis_size(('group', 'helper'))),...  7.45 us
    unnamed x24, local copies, waits for them, and re-layouts  6.32 us
    dot_general x1, matrix products, shards(): jnp.dot(normed, proj_full, preferred_element_type=jnp.float32)  5.88 us
  transfers between devices with their start and end apart: 4, of which 3 were waited for; matrix products, arithmetic and copies ran while one was open for 9% of the time, Pallas kernels for 0%

profile of v1, /device:TPU:0, one launch (start us, length us, event | category | flops | bytes accessed | tf_op | source)
XLA Modules:
  0.0 283.5 jit_solution(5538355818440011207)
XLA Ops:
  7.2 5.2 %stack.2 = bf16[32,32,4096]{2,1,0:T(8,128)(2,1)} broadcast(bf16[32,4096]{1,0:T(8,128)(2,1)} %param.15), dimensions={1,2} | broadcast | bytes 8650752 | tf_op jit(solution)/shard_map/stack | solution.py:36
  12.4 7.5 %all-to-all-start = ((bf16[32,32,4096]{2,1,0:T(8,128)(2,1)}), bf16[32,32,4096]{2,1,0:T(8,128)(2,1)}, u32[]{:S(2)}, u32[]{:S(2)}) async-start(bf16[32,32,4096]{2,1,0:T(8,128)(2,1)} %stack.2), calls=%async_computation | async-start | bytes 16777216 | tf_op jit(solution)/shard_map/all_to_all | solution.py:35
  19.8 0.0 all-gather.2.cloned.1.call-start
  19.9 0.7 all-gather.2.cloned.1.call-update
  20.6 0.0 copy-done
  20.6 0.1 convert_reduce_fusion
  20.7 0.3 multiply_reduce_fusion.3
  21.0 0.0 copy-done.4
  21.0 0.3 multiply_convert_fusion.1
  21.3 193.9 %all-to-all-done = bf16[32,32,4096]{2,1,0:T(8,128)(2,1)} async-done(((bf16[32,32,4096]{2,1,0:T(8,128)(2,1)}), bf16[32,32,4096]{2,1,0:T(8,128)(2,1)}, u32[]{:S(2)}, u32[]{:S(2)}) %all-to-all-start) | async-done | bytes 8388640 | tf_op jit(solution)/shard_map/all_to_all | solution.py:35
  215.3 5.9 %divide_multiply_fusion = f32[256,4096]{1,0:T(8,128)S(1)} fusion(bf16[256,1024]{1,0:T(8,128)(2,1)S(1)} %bitcast.49, bf16[1024,4096]{1,0:T(8,128)(2,1)} %bitcast.2), kind=kOutput, calls=%fused_computation.2 | convolution fusion | flops 2151677952 | bytes 13107200 | tf_op jit(solution)/shard_map/dot_general | solution.py:44
  221.2 1.9 copy-done.1
  223.1 0.1 slice.30
  223.2 0.4 reshape.119
  223.6 0.0 copy-start.2
  223.6 0.0 copy-start.3
  223.6 0.7 convolution_convert_fusion
  224.3 1.3 copy.47
  225.6 3.5 %all-to-all-start.1 = ((bf16[4,128,1024]{2,1,0:T(8,128)(2,1)}), bf16[4,128,1024]{2,1,0:T(8,128)(2,1)S(1)}, u32[]{:S(2)}, u32[]{:S(2)}) async-start(bf16[4,128,1024]{2,1,0:T(8,128)(2,1)} %bitcast.37), calls=%async_computation.1 | async-start | bytes 2097152 | tf_op jit(solution)/shard_map/all_to_all | solution.py:76
  229.1 0.9 copy.31
  230.0 0.0 copy-done.3
  230.0 0.9 copy.32
  230.9 11.8 %all-to-all-done.1 = bf16[4,128,1024]{2,1,0:T(8,128)(2,1)S(1)} async-done(((bf16[4,128,1024]{2,1,0:T(8,128)(2,1)}), bf16[4,128,1024]{2,1,0:T(8,128)(2,1)S(1)}, u32[]{:S(2)}, u32[]{:S(2)}) %all-to-all-start.1) | async-done | bytes 1048608 | tf_op jit(solution)/shard_map/all_to_all | solution.py:76
  242.7 0.3 copy.30
  243.0 4.0 %fusion.2 = bf16[512,8,128]{2,0,1:T(8,128)(2,1)} fusion(bf16[512,8,128]{2,1,0:T(8,128)(2,1)S(1)} %bitcast.44, bf16[256,8,128]{2,1,0:T(8,128)(2,1)} %bitcast.51, bf16[256,8,128]{2,1,0:T(8,128)(2,1)} %bitcast.50), kind=kOutput, calls=%fused_computation.5 | convolution fusion | flops 543686656 | bytes 3145728 | tf_op jit(solution)/shard_map/txw,wta->xta/dot_general | solution.py:72
  247.0 1.9 copy.26
  248.9 1.3 reshape.122
  250.2 3.7 %all-to-all-start.2 = ((bf16[4,128,1024]{2,1,0:T(8,128)(2,1)}), bf16[4,128,1024]{2,1,0:T(8,128)(2,1)S(1)}, u32[]{:S(2)}, u32[]{:S(2)}) async-start(bf16[4,128,1024]{2,1,0:T(8,128)(2,1)} %reshape.122), calls=%async_computation.2 | async-start | bytes 2097152 | tf_op jit(solution)/shard_map/all_to_all | solution.py:86
  253.9 1.4 fusion.5
  255.2 0.2 copy.34
  255.4 0.3 reduce_sum.74
  255.8 0.1 copy.27
  255.9 0.1 copy.28
  256.0 10.8 %all-to-all-done.2 = bf16[4,128,1024]{2,1,0:T(8,128)(2,1)S(1)} async-done(((bf16[4,128,1024]{2,1,0:T(8,128)(2,1)}), bf16[4,128,1024]{2,1,0:T(8,128)(2,1)S(1)}, u32[]{:S(2)}, u32[]{:S(2)}) %all-to-all-start.2) | async-done | bytes 1048608 | tf_op jit(solution)/shard_map/all_to_all | solution.py:86
  266.8 0.8 copy.33
  267.6 1.1 fusion.15
  268.7 0.0 copy-start.5
  268.7 0.9 reshape.124
  269.6 0.3 mul.126
  270.0 1.6 fusion.20
  271.5 0.2 multiply_reduce_fusion.2
  271.8 0.0 all-gather.2.cloned.1.call-done
  271.9 0.0 copy-start.8
  271.9 2.8 fusion.22
  274.6 0.3 multiply_reduce_fusion.1
  274.9 0.0 copy-done.6
  274.9 1.1 multiply_reduce_fusion
  276.0 0.6 compare_select_fusion
  (16 shorter events, 0.1 us)
Async XLA Ops:
  12.4 8.2 %copy-start = (bf16[2,128,1024]{2,1,0:T(8,128)(2,1)S(1)}, bf16[2,128,1024]{2,1,0:T(8,128)(2,1)}, u32[]{:S(2)}) copy-start(bf16[2,128,1024]{2,1,0:T(8,128)(2,1)} %param.10) | copy-start | bytes 1572868
  12.4 8.7 %copy-start.4 = (f32[1024]{0:T(1024)S(1)}, f32[1024]{0:T(1024)}, u32[]{:S(2)}) copy-start(f32[1024]{0:T(1024)} %param.17) | copy-start | bytes 12292
  12.4 202.9 %all-to-all-start = ((bf16[32,32,4096]{2,1,0:T(8,128)(2,1)}), bf16[32,32,4096]{2,1,0:T(8,128)(2,1)}, u32[]{:S(2)}, u32[]{:S(2)}) async-start(bf16[32,32,4096]{2,1,0:T(8,128)(2,1)} %stack.2), calls=%async_computation | async-start | bytes 16777216 | tf_op jit(solution)/shard_map/all_to_all | solution.py:35
  19.8 252.0 %all-gather.2.cloned.1.call-start = ((), (), s32[]{:S(2)}) async-start(), calls=%async_computation.3 | async-start | bytes 2162688 | tf_op jit(solution)/shard_map/all_gather | solution.py:40
  215.3 8.3 %copy-start.7 = (s32[2]{0:T(128)S(1)}, s32[2]{0:T(128)}, u32[]{:S(2)}) copy-start(s32[2]{0:T(128)} %param.11) | copy-start | bytes 28
  221.2 1.9 copy-start.1
  223.6 5.5 %copy-start.2 = (bf16[1,256,1024]{2,1,0:T(8,128)(2,1)S(1)}, bf16[1,256,1024]{2,1,0:T(8,128)(2,1)}, u32[]{:S(2)}) copy-start(bf16[1,256,1024]{2,1,0:T(8,128)(2,1)} %param.13) | copy-start | bytes 1572868
  223.6 6.4 %copy-start.3 = (bf16[1,256,1024]{2,1,0:T(8,128)(2,1)S(1)}, bf16[1,256,1024]{2,1,0:T(8,128)(2,1)}, u32[]{:S(2)}) copy-start(bf16[1,256,1024]{2,1,0:T(8,128)(2,1)} %param.14) | copy-start | bytes 1572868
  225.6 17.1 %all-to-all-start.1 = ((bf16[4,128,1024]{2,1,0:T(8,128)(2,1)}), bf16[4,128,1024]{2,1,0:T(8,128)(2,1)S(1)}, u32[]{:S(2)}, u32[]{:S(2)}) async-start(bf16[4,128,1024]{2,1,0:T(8,128)(2,1)} %bitcast.37), calls=%async_computation.1 | async-start | bytes 2097152 | tf_op jit(solution)/shard_map/all_to_all | solution.py:76
  250.2 16.6 %all-to-all-start.2 = ((bf16[4,128,1024]{2,1,0:T(8,128)(2,1)}), bf16[4,128,1024]{2,1,0:T(8,128)(2,1)S(1)}, u32[]{:S(2)}, u32[]{:S(2)}) async-start(bf16[4,128,1024]{2,1,0:T(8,128)(2,1)} %reshape.122), calls=%async_computation.2 | async-start | bytes 2097152 | tf_op jit(solution)/shard_map/all_to_all | solution.py:86
  268.7 3.1 %copy-start.5 = (f32[1024]{0:T(1024)S(1)}, f32[1024]{0:T(1024)}, u32[]{:S(2)}) copy-start(f32[1024]{0:T(1024)} %param.18) | copy-start | bytes 12292
  271.5 3.4 %copy-start.6 = (f32[1024]{0:T(1024)S(1)}, f32[1024]{0:T(1024)}, u32[]{:S(2)}) copy-start(f32[1024]{0:T(1024)} %param.19) | copy-start | bytes 12292
  271.9 4.1 %copy-start.8 = (s32[2]{0:T(128)S(1)}, s32[2]{0:T(128)}, u32[]{:S(2)}) copy-start(s32[2]{0:T(128)} %param.12) | copy-start | bytes 28
Sparse Core Ops, SparseCore 0:
  23.5 106.0 all-gather.1
